TPU v7x, 32 devices: a whole 2x2x4 slice. The times are simulated.
32 devices in a mesh: dp: 4 (over x, y), tp: 8 (over z, core).
Axes of the slice: x: 2, y: 2, z: 4, core: 2. Of those that a mesh axis runs over, the one named last changes fastest.
Arguments:
- x: bfloat16 [256, 2048], P('dp'), parts along dimension 0
- k_cache: bfloat16 [256, 2048, 16, 128], P('dp', None, 'tp'), parts along dimension 0
- v_cache: bfloat16 [256, 2048, 16, 128], P('dp', None, 'tp'), parts along dimension 0
- gain_a: bfloat16 [2048], replicated
- wq: bfloat16 [2048, 2048], P(None, 'tp')
- wo: bfloat16 [2048, 2048], P('tp')
- gain_m: bfloat16 [2048], replicated
- w_gate: bfloat16 [2048, 8192], P(None, 'tp')
- w_up: bfloat16 [2048, 8192], P(None, 'tp')
- w_down: bfloat16 [8192, 2048], P('tp')
Outputs:
- output: bfloat16 [256, 2048], P('dp'), parts along dimension 0
There are 4 independent parts. A program takes and returns all parts, laid end to end along the dimension named above; an argument that names none is the same for every part.
All inputs are finite; a program needn't handle non-finite values.
Results may differ from a plain program's by a relative error of at most 0.017.
Values are sent between devices in bfloat16 or wider.
A program may use at most 2 GiB of HBM per device.

v0:
```python
import jax
import jax.numpy as jnp
from jax import lax
from jax.sharding import PartitionSpec as P

HEAD = 128
THETA = 10000


def normed(x, gain):
    wide = x.astype(jnp.float32)
    scale = lax.rsqrt(jnp.mean(wide * wide, -1, keepdims=True) + 1e-6)
    return (wide * scale * gain.astype(jnp.float32)).astype(jnp.bfloat16)


def turned(t, place, theta):
    half = t.shape[-1] // 2
    angle = place.astype(jnp.float32)[:, None] * theta ** (-jnp.arange(half, dtype=jnp.float32) / half)
    cos, sin = jnp.cos(angle)[:, None], jnp.sin(angle)[:, None]
    a, b = t[..., :half].astype(jnp.float32), t[..., half:].astype(jnp.float32)
    return jnp.concatenate([a * cos - b * sin, b * cos + a * sin], -1).astype(jnp.bfloat16)


def matmul(a, w):
    return jnp.dot(a, w, preferred_element_type=jnp.float32).astype(jnp.bfloat16)


def einsum(form, a, b):
    return jnp.einsum(form, a.astype(jnp.float32), b.astype(jnp.float32))


def seen_by(a, wq, k_cache, v_cache, head, theta):
    batch, cache, kv_heads = k_cache.shape[:3]
    place = jnp.full((batch,), cache - 1)
    q = turned(matmul(a, wq).reshape(batch, -1, head), place, theta).reshape(batch, kv_heads, -1, head)
    scores = einsum("bgsd,bugd->bgsu", q, k_cache) * head**-0.5
    weights = jax.nn.softmax(scores, -1).astype(jnp.bfloat16)
    return einsum("bgsu,bugd->bgsd", weights, v_cache).astype(jnp.bfloat16).reshape(batch, -1)


def hidden_of(b, w_gate, w_up):
    gate = jnp.dot(b, w_gate, preferred_element_type=jnp.float32)
    up = jnp.dot(b, w_up, preferred_element_type=jnp.float32)
    return (jax.nn.silu(gate) * up).astype(jnp.bfloat16)


def solution(mesh):
    def added(t, term):
        return (t.astype(jnp.float32) + lax.psum(term.astype(jnp.bfloat16), "tp").astype(jnp.float32)).astype(jnp.bfloat16)

    def step(x, k_cache, v_cache, gain_a, wq, wo, gain_m, w_gate, w_up, w_down):
        seen = seen_by(normed(x, gain_a), wq, k_cache, v_cache, HEAD, THETA)
        h = added(x, jnp.dot(seen, wo, preferred_element_type=jnp.float32))
        return added(h, jnp.dot(hidden_of(normed(h, gain_m), w_gate, w_up), w_down, preferred_element_type=jnp.float32))

    states, cache, columns, rows_of = P("dp", None), P("dp", None, "tp", None), P(None, "tp"), P("tp", None)
    return jax.shard_map(
        step,
        mesh=mesh,
        in_specs=(states, cache, cache, P(None), columns, rows_of, P(None), columns, columns, rows_of),
        out_specs=states,
        check_vma=False,
    )
```

profile of v0, /device:TPU:0, one launch (start us, length us, event | category | flops | bytes accessed | tf_op | source)
XLA Modules:
  0.0 203.3 jit_solution(18306614422506607042)
XLA Ops:
  6.5 0.0 copy-start
  6.5 0.0 all-reduce.3.cloned.1.call-start
  6.6 0.8 convert_element_type.66
  7.4 1.1 fusion.14
  8.5 1.7 convolution_convert_fusion.2
  10.2 0.1 fusion.51
  10.3 0.1 maximum_bitcast_fusion
  10.4 33.1 %fusion.4 = f32[64,2,1,2048]{3,2,1,0:T(1,128)S(1)} fusion(bf16[64,2048,2,128]{3,2,1,0:T(2,128)(2,1)} %param.11, bf16[64,2,128,1]{2,0,1,3:T(8,128)(2,1)S(1)} %maximum_bitcast_fusion), kind=kOutput, calls=%fused_computation.4 | convolution fusion | flops 67108864 | bytes 68190208 | tf_op jit(solution)/shard_map/bgsd,bugd->bgsu/dot_general | solution.py:29
  43.5 1.4 fusion.10
  44.9 0.0 copy-start.2
  44.9 0.0 copy-start.1
  44.9 25.9 %fusion.2 = f32[64,2,1,128]{3,2,1,0:T(1,128)S(1)} fusion(bf16[64,2048,2,128]{3,2,1,0:T(2,128)(2,1)} %param.12, bf16[64,2,2048,1]{2,0,1,3:T(8,128)(2,1)S(1)} %fusion.10), kind=kOutput, calls=%fused_computation.2 | convolution fusion | flops 67108864 | bytes 67698688 | tf_op jit(solution)/shard_map/bgsu,bugd->bgsd/dot_general | solution.py:29
  70.8 0.0 copy-done
  70.8 1.0 convolution_convert_fusion
  71.8 0.0 all-reduce.3.cloned.1.call-update
  71.9 0.0 all-reduce.5.cloned.1.call-start
  71.9 0.0 copy-done.2
  71.9 58.2 %all-reduce.3.cloned.1.call-done = bf16[64,2048]{1,0:T(8,128)(2,1)} async-done(((bf16[64,2048]{1,0:T(8,128)(2,1)}), bf16[64,2048]{1,0:T(8,128)(2,1)}) %all-reduce.3.cloned.1.call-update) | async-done | bytes 262160 | tf_op jit(solution)/shard_map/psum | solution.py:49
  130.1 0.0 copy-done.1
  130.1 1.1 fusion.18
  131.3 3.1 %fusion.34 = f32[64,1024]{1,0:T(8,128)S(1)} fusion(bf16[2048,1024]{1,0:T(8,128)(2,1)} %param.17, bf16[64,2048]{1,0:T(8,128)(2,1)S(1)} %get-tuple-element.6, f32[2048]{0:T(1024)S(1)} %convert_element_type.77, f32[64]{0:T(128)S(1)} %add_rsqrt_fusion), kind=kOutput, calls=%fused_computation.46 | convolution fusion | flops 268959744 | bytes 4727040 | tf_op jit(solution)/shard_map/dot_general | solution.py:42
  134.4 5.8 %convolution_convert_fusion.1 = bf16[64,2048]{1,0:T(8,128)(2,1)} fusion(bf16[1024,2048]{1,0:T(8,128)(2,1)} %param.19, bf16[2048,1024]{1,0:T(8,128)(2,1)} %param.18, f32[64,1024]{1,0:T(8,128)S(1)} %fusion.34, bf16[64,2048]{1,0:T(8,128)(2,1)S(1)} %get-tuple-element.6, f32[2048]{0:T(1024)S(1)} %convert_element_type.77, f32[64]{0:T(128)S(1)} %add_rsqrt_fusion), kind=kOutput, calls=%fused_computation.12 | convolution fusion | flops 537919488 | bytes 9183488 | tf_op jit(solution)/shard_map/dot_general | solution.py:54
  140.2 0.0 all-reduce.5.cloned.1.call-update
  140.2 54.5 %all-reduce.5.cloned.1.call-done = bf16[64,2048]{1,0:T(8,128)(2,1)} async-done(((bf16[64,2048]{1,0:T(8,128)(2,1)}), bf16[64,2048]{1,0:T(8,128)(2,1)}) %all-reduce.5.cloned.1.call-update) | async-done | bytes 262160 | tf_op jit(solution)/shard_map/psum | solution.py:49
  194.7 1.7 fusion.21
  (7 shorter events, 0.1 us)
Async XLA Ops:
  6.5 64.3 %copy-start = (bf16[256,2048]{1,0:T(8,128)(2,1)S(1)}, bf16[256,2048]{1,0:T(8,128)(2,1)}, u32[]{:S(2)}) copy-start(bf16[256,2048]{1,0:T(8,128)(2,1)} %param.15) | copy-start | bytes 3145732
  6.5 123.6 %all-reduce.3.cloned.1.call-start = ((), (), s32[]{:S(2)}) async-start(), calls=%async_computation | async-start | bytes 524288 | tf_op jit(solution)/shard_map/psum | solution.py:49
  44.9 27.0 %copy-start.2 = (bf16[2048]{0:T(1024)(128)(2,1)S(1)}, bf16[2048]{0:T(1024)(128)(2,1)}, u32[]{:S(2)}) copy-start(bf16[2048]{0:T(1024)(128)(2,1)} %param.16) | copy-start | bytes 12292
  44.9 85.2 %copy-start.1 = (bf16[64,2048]{1,0:T(8,128)(2,1)S(1)}, bf16[64,2048]{1,0:T(8,128)(2,1)}, u32[]{:S(2)}) copy-start(bf16[64,2048]{1,0:T(8,128)(2,1)} %param.10) | copy-start | bytes 786436
  71.9 122.9 %all-reduce.5.cloned.1.call-start = ((), (), s32[]{:S(2)}) async-start(), calls=%async_computation.1 | async-start | bytes 524288 | tf_op jit(solution)/shard_map/psum | solution.py:49
Sparse Core Ops, SparseCore 0:
  72.0 58.1 all-reduce.2
  140.3 54.3 all-reduce.4
where the time goes:
time: 204 us; the launch traced here: 203 us
  waiting for transfers between devices  113 us (55%)
  matrix products  70.5 us (35%)
  between operations  13.5 us (7%)
  other arithmetic  6.35 us (3%)
    psum x2, waiting for transfers between devices, added(): lax.psum(term.astype(jnp.bfloat16), 'tp').astype(jnp.float32)  113 us
    dot_general x2, matrix products, einsum(): return jnp.einsum(form, a.astype(jnp.float32), b.astype(jnp.float32))  58.9 us
    dot_general x1, matrix products, step(): jnp.dot(hidden_of(normed(h, gain_m), w_gate, w_up), w_down, preferred_ele...  5.81 us
  transfers between devices with their start and end apart: 2, of which 2 were waited for; matrix products, arithmetic and copies ran while one was open for 0% of the time, Pallas kernels for 0%

commit v1 on v0

v1 whole, which is shorter than its diff:
```python
import jax
import jax.numpy as jnp
import numpy as np
from jax import lax
from jax.experimental import pallas as pl
from jax.experimental.pallas import tpu as pltpu
from jax.sharding import PartitionSpec as P

HEAD = 128
THETA = 10000
ROWS = 64
CACHE = 2048
D = 2048
HALF = D // 2
FF = 1024
KEYS = 2 * CACHE
PAIRS = ROWS // 2
SLOTS = 8
CHUNK = 16
STEP = CHUNK // 2
CHUNKS = ROWS // CHUNK
TILE = 256
TILES = KEYS // TILE
AT = (0, 1, 4, 5, 6, 9, 10)
F32, BF16 = jnp.float32, jnp.bfloat16


def dot(a, b):
    return jnp.dot(a, b, preferred_element_type=F32)


def wide_norm(wide, gain):
    scale = lax.rsqrt(jnp.mean(wide * wide, -1, keepdims=True) + 1e-6)
    return (wide * scale * gain).astype(BF16)


def one_hot(shape, hit):
    row, column = lax.broadcasted_iota(jnp.int32, shape, 0), lax.broadcasted_iota(jnp.int32, shape, 1)
    return jnp.where(hit(row, column), 1.0, 0.0).astype(BF16)


def kernel(x_in, k_in, v_in, ga_in, wq_in, wo_in, gm_in, wg_in, wu_in, wd_in, turn_in, y_out,
           x, kbuf, vbuf, ga, gm, turn, wq, wo, wg, wu, wd, queries, weights, results, hidden, term,
           sent, paired, summed, h, y, ksem, vsem, lsem, osem, pair_s, pair_r, z_s, z_r, done_s, done_r):
    me = lax.axis_index("tp")
    z, core = me // 2, me % 2
    partner = z * 2 + 1 - core

    def load_k(i, slot):
        return pltpu.make_async_copy(k_in.at[pl.ds(2 * i, 2)], kbuf.at[slot], ksem.at[slot])

    def load_v(i, slot):
        return pltpu.make_async_copy(v_in.at[pl.ds(2 * i, 2)], vbuf.at[slot], vsem.at[slot])

    first = [pltpu.make_async_copy(src, dst, lsem.at[n]) for n, (src, dst) in enumerate((
        (x_in.at[:, pl.ds(0, HALF)], x.at[0]), (x_in.at[:, pl.ds(HALF, HALF)], x.at[1]), (ga_in, ga), (turn_in, turn), (wq_in, wq)))]
    later = [pltpu.make_async_copy(src, dst, lsem.at[len(first) + n]) for n, (src, dst) in enumerate((
        (gm_in, gm), (wo_in, wo), (wg_in, wg), (wu_in, wu), (wd_in, wd)))]
    for copy in first:
        copy.start()
    for i in range(SLOTS):
        load_k(i, i).start()
        load_v(i, i).start()

    barrier = pltpu.get_barrier_semaphore()
    others = [lax.rem(z + n, 4) for n in (1, 2, 3)]
    for peer in [partner] + [2 * other + core for other in others]:
        pl.semaphore_signal(barrier, inc=1, device_id={"tp": peer}, device_id_type=pl.DeviceIdType.MESH)

    def gain_row(ref):
        wide = ref[...].astype(F32)
        return jnp.concatenate([wide[n:n + 1, :] for n in range(D // 128)], axis=1)

    for copy in first:
        copy.wait()
    a = wide_norm(jnp.concatenate([x[0], x[1]], axis=1).astype(F32), gain_row(ga))
    q = dot(a, wq[...]).astype(BF16).astype(F32)
    cos, sin = turn[0:1, :], turn[1:2, :]
    heads = [q[:, n * HEAD:(n + 1) * HEAD] for n in range(2)]
    stacked = jnp.concatenate([(t * cos + pltpu.roll(t, HEAD // 2, 1) * sin).astype(BF16) for t in heads], axis=0)
    left = one_hot((16 * PAIRS, 2 * ROWS), lambda r, c: (r % 16 == c // ROWS) & (c % ROWS == 2 * (r // 16)))
    right = one_hot((16 * PAIRS, 2 * ROWS), lambda r, c: (r % 16 == 2 + c // ROWS) & (c % ROWS == 2 * (r // 16) + 1))
    queries[:, 0:HEAD] = dot(left, stacked).astype(BF16)
    queries[:, HEAD:] = dot(right, stacked).astype(BF16)

    own = lax.broadcasted_iota(jnp.int32, (8, TILE), 0) % 2 == lax.broadcasted_iota(jnp.int32, (8, TILE), 1) % 2

    def scores(i, slot):
        pair = queries[pl.ds(pl.multiple_of(16 * i, 16), 16), :]
        out = []
        for t in range(TILES):
            at = pl.ds(t * TILE, TILE)
            keys = jnp.concatenate([kbuf[slot, 0, at, :], kbuf[slot, 1, at, :]], axis=1)
            s = lax.dot_general(pair, keys, (((1,), (1,)), ((), ())), preferred_element_type=F32)[0:8]
            out.append(jnp.where(own, s * HEAD**-0.5, -jnp.inf))
        return out

    def softmax(s):
        top = s[0]
        for t in s[1:]:
            top = jnp.maximum(top, t)
        top = jnp.max(top, -1, keepdims=True)
        e = [jnp.exp(t - top) for t in s]
        total = e[0]
        for t in e[1:]:
            total = total + t
        scale = 1.0 / jnp.sum(total, -1, keepdims=True)
        blank = jnp.zeros((8, TILE), F32)
        for t in range(TILES):
            weights[:, t * TILE:(t + 1) * TILE] = jnp.concatenate([e[t] * scale, blank], axis=0).astype(BF16)

    def values(i, slot):
        parts = [None, None]
        for t in range(TILES):
            at = pl.ds(t * TILE, TILE)
            v = jnp.concatenate([vbuf[slot, 0, at, :], vbuf[slot, 1, at, :]], axis=1)
            p = dot(weights[:, t * TILE:(t + 1) * TILE], v)
            parts[t % 2] = p if parts[t % 2] is None else parts[t % 2] + p
        results[pl.ds(pl.multiple_of(8 * i, 8), 8), :] = (parts[0] + parts[1])[0:8]

    load_k(0, 0).wait()
    softmax(scores(0, 0))
    load_k(SLOTS, 0).start()
    for copy in later:
        copy.start()

    pl.semaphore_wait(barrier, 4)

    def to_partner(src, dst, send, recv):
        return pltpu.make_async_remote_copy(src, dst, send, recv, device_id={"tp": partner}, device_id_type=pl.DeviceIdType.MESH)

    def to_chip(n, rnd, c, rows):
        return pltpu.make_async_remote_copy(
            summed.at[rnd, z, rows], summed.at[rnd, z, rows], z_s.at[rnd, c, n], z_r.at[rnd, c, z],
            device_id={"tp": 2 * others[n] + core}, device_id_type=pl.DeviceIdType.MESH)

    def from_chip(n, rnd, c, rows):
        other = others[n]
        return pltpu.make_async_remote_copy(
            summed.at[rnd, other, rows], summed.at[rnd, other, rows], z_s.at[rnd, c, n], z_r.at[rnd, c, other],
            device_id={"tp": 2 * other + core}, device_id_type=pl.DeviceIdType.MESH)

    def first_leg(rnd, c, rows):
        return to_partner(sent.at[rnd, rows], paired.at[rnd, rows], pair_s.at[rnd, c], pair_r.at[rnd, c])

    def send_term(rnd, c, rows):
        sent[rnd, rows, :] = term[rnd, 1 - core].astype(BF16)
        first_leg(rnd, c, rows).start()

    def second_leg(rnd, c, rows):
        first_leg(rnd, c, rows).wait()
        summed[rnd, z, rows, :] = (term[rnd, core] + paired[rnd, rows, :].astype(F32)).astype(BF16)
        for n in range(3):
            to_chip(n, rnd, c, rows).start()

    def third_leg(rnd, c, rows, base, out):
        for n in range(3):
            to_chip(n, rnd, c, rows).wait_send()
            from_chip(n, rnd, c, rows).wait_recv()
        total = summed[rnd, 0, rows, :].astype(F32)
        for n in range(1, 4):
            total = total + summed[rnd, n, rows, :].astype(F32)
        out[core, rows, :] = (base[core, rows, :].astype(F32) + total).astype(BF16)
        to_partner(out.at[core, rows], out.at[core, rows], done_s.at[rnd, c], done_r.at[rnd, c]).start()

    def finished(rnd, c, rows, out):
        to_partner(out.at[core, rows], out.at[core, rows], done_s.at[rnd, c], done_r.at[rnd, c]).wait_send()
        to_partner(out.at[1 - core, rows], out.at[1 - core, rows], done_s.at[rnd, c], done_r.at[rnd, c]).wait_recv()

    def project(c, rows):
        @pl.when(c == 0)
        def _():
            later[0].wait()
            later[1].wait()

        got = results[pl.ds(pl.multiple_of(8 * STEP * c, 8 * STEP), 8 * STEP), :].astype(BF16)
        seen = []
        for g in range(2):
            even = one_hot((CHUNK, 8 * STEP), lambda r, k: (r % 2 == 0) & (k == 8 * (r // 2) + g))
            odd = one_hot((CHUNK, 8 * STEP), lambda r, k: (r % 2 == 1) & (k == 8 * (r // 2) + 2 + g))
            seen.append((dot(even, got[:, 0:HEAD]) + dot(odd, got[:, HEAD:])).astype(BF16))
        seen = jnp.concatenate(seen, axis=1)
        for n in range(2):
            term[0, n] = dot(seen, wo[:, n * HALF:(n + 1) * HALF])
        send_term(0, c, rows)

    def mlp(c, rows):
        @pl.when(c == 0)
        def _():
            for copy in later[2:]:
                copy.wait()

        finished(0, c, rows, h)
        b = wide_norm(jnp.concatenate([h[0, rows, :], h[1, rows, :]], axis=1).astype(F32), gain_row(gm))

        @pl.loop(0, 2)
        def _(n):
            at = pl.ds(pl.multiple_of(n * (FF // 2), FF // 2), FF // 2)
            gate = dot(b, wg[:, at])
            hidden[:, at] = (gate * jax.nn.sigmoid(gate) * dot(b, wu[:, at])).astype(BF16)

        @pl.loop(0, 2)
        def _(n):
            term[1, n] = dot(hidden[...], wd[:, pl.ds(pl.multiple_of(n * HALF, HALF), HALF)])

        send_term(1, c, rows)

    def out_copy(n, c, rows):
        return pltpu.make_async_copy(y.at[n, rows], y_out.at[rows, pl.ds(n * HALF, HALF)], osem.at[n, c])

    def write(c, rows):
        finished(1, c, rows, y)
        for n in range(2):
            out_copy(n, c, rows).start()

    stages = (project, lambda c, rows: second_leg(0, c, rows), lambda c, rows: third_leg(0, c, rows, x, h), mlp,
              lambda c, rows: second_leg(1, c, rows), lambda c, rows: third_leg(1, c, rows, h, y), write)

    def iteration(i, _):
        @pl.when(i < PAIRS)
        def _():
            slot, before = i % SLOTS, (i - 1) % SLOTS
            load_k(i, slot).wait()
            load_v(i - 1, before).wait()
            s = scores(i, slot)
            values(i - 1, before)
            softmax(s)

            @pl.when(i + SLOTS < PAIRS)
            def _():
                load_k(i + SLOTS, slot).start()

            @pl.when(i - 1 + SLOTS < PAIRS)
            def _():
                load_v(i - 1 + SLOTS, before).start()

        @pl.when(i == PAIRS)
        def _():
            load_v(PAIRS - 1, (PAIRS - 1) % SLOTS).wait()
            values(PAIRS - 1, (PAIRS - 1) % SLOTS)

        for stage, at in zip(stages, AT):
            since = i - STEP - at

            @pl.when((since >= 0) & (since < STEP * CHUNKS) & (since % STEP == 0))
            def _():
                c = since // STEP
                stage(c, pl.ds(pl.multiple_of(c * CHUNK, CHUNK), CHUNK))

        return 0

    lax.fori_loop(1, PAIRS + AT[-1] + 1, iteration, 0)
    for c in range(CHUNKS):
        for n in range(2):
            out_copy(n, c, pl.ds(c * CHUNK, CHUNK)).wait()


def turn_table():
    angle = (CACHE - 1) * float(THETA) ** (-np.arange(HEAD // 2) / (HEAD // 2))
    cos, sin = np.cos(angle), np.sin(angle)
    table = np.zeros((8, HEAD), np.float32)
    table[0] = np.concatenate([cos, cos])
    table[1] = np.concatenate([-sin, sin])
    return table


def solution(mesh):
    def step(x, k_cache, v_cache, gain_a, wq, wo, gain_m, w_gate, w_up, w_down):
        dma, vmem = pltpu.SemaphoreType.DMA, pltpu.VMEM
        return pl.pallas_call(
            kernel,
            out_shape=jax.ShapeDtypeStruct((ROWS, D), BF16),
            in_specs=[pl.BlockSpec(memory_space=pl.ANY)] * 11,
            out_specs=pl.BlockSpec(memory_space=pl.ANY),
            scratch_shapes=[
                vmem((2, ROWS, HALF), BF16),
                vmem((SLOTS, 2, KEYS, HEAD), BF16), vmem((SLOTS, 2, KEYS, HEAD), BF16),
                vmem((D // 128, 128), BF16), vmem((D // 128, 128), BF16), vmem((8, HEAD), F32),
                vmem((D, 2 * HEAD), BF16), vmem((2 * HEAD, D), BF16), vmem((D, FF), BF16), vmem((D, FF), BF16), vmem((FF, D), BF16),
                vmem((16 * PAIRS, 2 * HEAD), BF16), vmem((16, KEYS), BF16), vmem((8 * PAIRS, 2 * HEAD), F32), vmem((CHUNK, FF), BF16),
                vmem((2, 2, CHUNK, HALF), F32),
                vmem((2, ROWS, HALF), BF16), vmem((2, ROWS, HALF), BF16), vmem((2, 4, ROWS, HALF), BF16),
                vmem((2, ROWS, HALF), BF16), vmem((2, ROWS, HALF), BF16),
                dma((SLOTS,)), dma((SLOTS,)), dma((10,)), dma((2, CHUNKS)),
                dma((2, CHUNKS)), dma((2, CHUNKS)), dma((2, CHUNKS, 3)), dma((2, CHUNKS, 4)), dma((2, CHUNKS)), dma((2, CHUNKS)),
            ],
            compiler_params=pltpu.CompilerParams(collective_id=0, has_side_effects=True, vmem_limit_bytes=60 * 2**20),
            name="layer",
        )(x, k_cache.reshape(ROWS, KEYS, HEAD), v_cache.reshape(ROWS, KEYS, HEAD), gain_a.reshape(D // 128, 128), wq, wo,
          gain_m.reshape(D // 128, 128), w_gate, w_up, w_down, jnp.asarray(turn_table()))

    states, cache, columns, rows_of = P("dp", None), P("dp", None, "tp", None), P(None, "tp"), P("tp", None)
    return jax.shard_map(
        step,
        mesh=mesh,
        in_specs=(states, cache, cache, P(None), columns, rows_of, P(None), columns, columns, rows_of),
        out_specs=states,
        check_vma=False,
    )
```

time: 204 us -> 82.7 us (0.41)
  waiting for transfers between devices: 113 us -> 0 us
  Pallas kernels: 0 us -> 80.9 us
  matrix products: 70.5 us -> 0 us
  between operations: 13.5 us -> 0.01 us
  other arithmetic: 6.35 us -> 0 us
    psum x2 -> x0, waiting for transfers between devices: 113 us -> none  [added(): lax.psum(term.astype(jnp.bfloat16), 'tp').astype(jnp.float32)]
    pallas_call x0 -> x1, Pallas kernels: none -> 80.9 us  [step(): pl.pallas_call(kernel, out_shape=jax.ShapeDtypeStruct((ROWS, D), BF16), i...]
    dot_general x6 -> x0, matrix products: 70.5 us -> none  [the longest x2 58.9 us: einsum(): return jnp.einsum(form, a.astype(jnp.float32), b.astype(jnp.float32))]
    convert_element_type x4 -> x0, other arithmetic: 2.51 us -> none  [the longest x1 1.71 us: added(): (t.astype(jnp.float32) + lax.psum(term.astype(jnp.bfloat16), 'tp').astype...]
    reduce_sum x2 -> x0, other arithmetic: 2.24 us -> none  [normed(): scale = lax.rsqrt(jnp.mean(wide * wide, -1, keepdims=True) + 1e-06)]
  transfers between devices with their start and end apart: 2 -> 0, of which waited for: 2 -> 0; matrix products, arithmetic and copies ran while one was open for 0% -> 0% of each run, Pallas kernels for 0% -> 0%
where the time goes in v1:
time: 82.7 us; the launch traced here: 82.6 us
  Pallas kernels  80.9 us (98%)
  local copies, waits for them, and re-layouts  1.67 us (2%)
    pallas_call x1, Pallas kernels, step(): pl.pallas_call(kernel, out_shape=jax.ShapeDtypeStruct((ROWS, D), BF16), i...  80.9 us
    unnamed x1, local copies, waits for them, and re-layouts  1.67 us

profile of v1, /device:TPU:0, one launch (start us, length us, event | category | flops | bytes accessed | tf_op | source)
XLA Modules:
  0.0 82.6 jit_solution(11901320724345277562)
XLA Ops:
  0.0 80.9 %layer.1 = bf16[64,2048]{1,0:T(8,128)(2,1)} custom-call(bf16[64,2048]{1,0:T(8,128)(2,1)} %x_in.1, bf16[64,4096,128]{2,1,0:T(8,128)(2,1)} %bitcast.k_in, bf16[64,4096,128]{2,1,0:T(8,128)(2,1)} %bitcast.1.v_in, bf16[16,128]{1,0:T(8,128)(2,1)} %bitcast.4, bf16[2048,256]{1,0:T(8,128)(2,1)} %wq_in.1, bf16[256,2048]{1,0:T(8,128)(2,1)} %wo_in.1, ...), custom_call_target="tpu_custom_call" | custom-call | tf_op jit(solution)/shard_map/layer/pallas_call | solution.py:270
  80.9 1.7 %copy.13 = bf16[64,2048]{1,0:T(8,128)(2,1)} copy(bf16[64,2048]{1,0:T(8,128)(2,1)} %layer.1) | data formatting | bytes 524288

commit v2 on v1

--- a/solution.py
+++ b/solution.py
@@ -21,7 +21,7 @@
 CHUNKS = ROWS // CHUNK
 TILE = 256
 TILES = KEYS // TILE
-AT = (0, 1, 4, 5, 6, 9, 10)
+AT = (0, 1, 7, 9, 10, 16, 17)
 F32, BF16 = jnp.float32, jnp.bfloat16
 
 
@@ -40,7 +40,7 @@
 
 
 def kernel(x_in, k_in, v_in, ga_in, wq_in, wo_in, gm_in, wg_in, wu_in, wd_in, turn_in, y_out,
-           x, kbuf, vbuf, ga, gm, turn, wq, wo, wg, wu, wd, queries, weights, results, hidden, term,
+           x, kbuf, vbuf, ga, gm, turn, wq, wo, wg, wu, wd, queries, logits, weights, results, term,
            sent, paired, summed, h, y, ksem, vsem, lsem, osem, pair_s, pair_r, z_s, z_r, done_s, done_r):
     me = lax.axis_index("tp")
     z, core = me // 2, me % 2
@@ -87,15 +87,14 @@
 
     def scores(i, slot):
         pair = queries[pl.ds(pl.multiple_of(16 * i, 16), 16), :]
-        out = []
         for t in range(TILES):
             at = pl.ds(t * TILE, TILE)
             keys = jnp.concatenate([kbuf[slot, 0, at, :], kbuf[slot, 1, at, :]], axis=1)
             s = lax.dot_general(pair, keys, (((1,), (1,)), ((), ())), preferred_element_type=F32)[0:8]
-            out.append(jnp.where(own, s * HEAD**-0.5, -jnp.inf))
-        return out
-
-    def softmax(s):
+            logits[:, t * TILE:(t + 1) * TILE] = jnp.where(own, s * HEAD**-0.5, -jnp.inf)
+
+    def softmax():
+        s = [logits[:, t * TILE:(t + 1) * TILE] for t in range(TILES)]
         top = s[0]
         for t in s[1:]:
             top = jnp.maximum(top, t)
@@ -106,8 +105,11 @@
             total = total + t
         scale = 1.0 / jnp.sum(total, -1, keepdims=True)
         blank = jnp.zeros((8, TILE), F32)
+        return [jnp.concatenate([t * scale, blank], axis=0).astype(BF16) for t in e]
+
+    def keep(w):
         for t in range(TILES):
-            weights[:, t * TILE:(t + 1) * TILE] = jnp.concatenate([e[t] * scale, blank], axis=0).astype(BF16)
+            weights[:, t * TILE:(t + 1) * TILE] = w[t]
 
     def values(i, slot):
         parts = [None, None]
@@ -119,10 +121,14 @@
         results[pl.ds(pl.multiple_of(8 * i, 8), 8), :] = (parts[0] + parts[1])[0:8]
 
     load_k(0, 0).wait()
-    softmax(scores(0, 0))
-    load_k(SLOTS, 0).start()
+    scores(0, 0)
     for copy in later:
         copy.start()
+    load_k(SLOTS, 0).start()
+    load_k(1, 1).wait()
+    keep(softmax())
+    scores(1, 1)
+    load_k(SLOTS + 1, 1).start()
 
     pl.semaphore_wait(barrier, 4)
 
@@ -143,13 +149,17 @@
     def first_leg(rnd, c, rows):
         return to_partner(sent.at[rnd, rows], paired.at[rnd, rows], pair_s.at[rnd, c], pair_r.at[rnd, c])
 
-    def send_term(rnd, c, rows):
-        sent[rnd, rows, :] = term[rnd, 1 - core].astype(BF16)
+    def send_term(rnd, c, rows, left, w):
+        def half(n):
+            return dot(left, w[:, pl.ds(pl.multiple_of(n * HALF, HALF), HALF)])
+
+        sent[rnd, rows, :] = half(1 - core).astype(BF16)
         first_leg(rnd, c, rows).start()
+        term[rnd] = half(core)
 
     def second_leg(rnd, c, rows):
         first_leg(rnd, c, rows).wait()
-        summed[rnd, z, rows, :] = (term[rnd, core] + paired[rnd, rows, :].astype(F32)).astype(BF16)
+        summed[rnd, z, rows, :] = (term[rnd] + paired[rnd, rows, :].astype(F32)).astype(BF16)
         for n in range(3):
             to_chip(n, rnd, c, rows).start()
 
@@ -180,9 +190,7 @@
             odd = one_hot((CHUNK, 8 * STEP), lambda r, k: (r % 2 == 1) & (k == 8 * (r // 2) + 2 + g))
             seen.append((dot(even, got[:, 0:HEAD]) + dot(odd, got[:, HEAD:])).astype(BF16))
         seen = jnp.concatenate(seen, axis=1)
-        for n in range(2):
-            term[0, n] = dot(seen, wo[:, n * HALF:(n + 1) * HALF])
-        send_term(0, c, rows)
+        send_term(0, c, rows, seen, wo)
 
     def mlp(c, rows):
         @pl.when(c == 0)
@@ -193,17 +201,12 @@
         finished(0, c, rows, h)
         b = wide_norm(jnp.concatenate([h[0, rows, :], h[1, rows, :]], axis=1).astype(F32), gain_row(gm))
 
-        @pl.loop(0, 2)
-        def _(n):
-            at = pl.ds(pl.multiple_of(n * (FF // 2), FF // 2), FF // 2)
-            gate = dot(b, wg[:, at])
-            hidden[:, at] = (gate * jax.nn.sigmoid(gate) * dot(b, wu[:, at])).astype(BF16)
-
-        @pl.loop(0, 2)
-        def _(n):
-            term[1, n] = dot(hidden[...], wd[:, pl.ds(pl.multiple_of(n * HALF, HALF), HALF)])
-
-        send_term(1, c, rows)
+        part = FF // 4
+        hidden = []
+        for n in range(4):
+            gate = dot(b, wg[:, n * part:(n + 1) * part])
+            hidden.append((gate * jax.nn.sigmoid(gate) * dot(b, wu[:, n * part:(n + 1) * part])).astype(BF16))
+        send_term(1, c, rows, jnp.concatenate(hidden, axis=1), wd)
 
     def out_copy(n, c, rows):
         return pltpu.make_async_copy(y.at[n, rows], y_out.at[rows, pl.ds(n * HALF, HALF)], osem.at[n, c])
@@ -219,28 +222,34 @@
     def iteration(i, _):
         @pl.when(i < PAIRS)
         def _():
-            slot, before = i % SLOTS, (i - 1) % SLOTS
+            slot, before = i % SLOTS, (i - 2) % SLOTS
             load_k(i, slot).wait()
-            load_v(i - 1, before).wait()
-            s = scores(i, slot)
-            values(i - 1, before)
-            softmax(s)
+            load_v(i - 2, before).wait()
+            values(i - 2, before)
+            keep(softmax())
+            scores(i, slot)
 
             @pl.when(i + SLOTS < PAIRS)
             def _():
                 load_k(i + SLOTS, slot).start()
 
-            @pl.when(i - 1 + SLOTS < PAIRS)
+            @pl.when(i - 2 + SLOTS < PAIRS)
             def _():
-                load_v(i - 1 + SLOTS, before).start()
+                load_v(i - 2 + SLOTS, before).start()
 
         @pl.when(i == PAIRS)
+        def _():
+            load_v(PAIRS - 2, (PAIRS - 2) % SLOTS).wait()
+            values(PAIRS - 2, (PAIRS - 2) % SLOTS)
+            keep(softmax())
+
+        @pl.when(i == PAIRS + 1)
         def _():
             load_v(PAIRS - 1, (PAIRS - 1) % SLOTS).wait()
             values(PAIRS - 1, (PAIRS - 1) % SLOTS)
 
         for stage, at in zip(stages, AT):
-            since = i - STEP - at
+            since = i - STEP - 1 - at
 
             @pl.when((since >= 0) & (since < STEP * CHUNKS) & (since % STEP == 0))
             def _():
@@ -249,7 +258,7 @@
 
         return 0
 
-    lax.fori_loop(1, PAIRS + AT[-1] + 1, iteration, 0)
+    lax.fori_loop(2, PAIRS + AT[-1] + 2, iteration, 0)
     for c in range(CHUNKS):
         for n in range(2):
             out_copy(n, c, pl.ds(c * CHUNK, CHUNK)).wait()
@@ -277,8 +286,8 @@
                 vmem((SLOTS, 2, KEYS, HEAD), BF16), vmem((SLOTS, 2, KEYS, HEAD), BF16),
                 vmem((D // 128, 128), BF16), vmem((D // 128, 128), BF16), vmem((8, HEAD), F32),
                 vmem((D, 2 * HEAD), BF16), vmem((2 * HEAD, D), BF16), vmem((D, FF), BF16), vmem((D, FF), BF16), vmem((FF, D), BF16),
-                vmem((16 * PAIRS, 2 * HEAD), BF16), vmem((16, KEYS), BF16), vmem((8 * PAIRS, 2 * HEAD), F32), vmem((CHUNK, FF), BF16),
-                vmem((2, 2, CHUNK, HALF), F32),
+                vmem((16 * PAIRS, 2 * HEAD), BF16), vmem((8, KEYS), F32), vmem((16, KEYS), BF16), vmem((8 * PAIRS, 2 * HEAD), F32),
+                vmem((2, CHUNK, HALF), F32),
                 vmem((2, ROWS, HALF), BF16), vmem((2, ROWS, HALF), BF16), vmem((2, 4, ROWS, HALF), BF16),
                 vmem((2, ROWS, HALF), BF16), vmem((2, ROWS, HALF), BF16),
                 dma((SLOTS,)), dma((SLOTS,)), dma((10,)), dma((2, CHUNKS)),

time: 82.7 us -> 70.1 us (0.85)
  Pallas kernels: 80.9 us -> 68.3 us
    pallas_call x1, Pallas kernels: 80.9 us -> 68.3 us  [step(): pl.pallas_call(kernel, out_shape=jax.ShapeDtypeStruct((ROWS, D), BF16), i...]
where the time goes in v2:
time: 70.1 us; the launch traced here: 69.9 us
  Pallas kernels  68.3 us (97%)
  local copies, waits for them, and re-layouts  1.67 us (2%)
    pallas_call x1, Pallas kernels, step(): pl.pallas_call(kernel, out_shape=jax.ShapeDtypeStruct((ROWS, D), BF16), i...  68.3 us
    unnamed x1, local copies, waits for them, and re-layouts  1.67 us

profile of v2, /device:TPU:0, one launch (start us, length us, event | category | flops | bytes accessed | tf_op | source)
XLA Modules:
  0.0 69.9 jit_solution(9236157670697201514)
XLA Ops:
  0.0 68.3 %layer.1 = bf16[64,2048]{1,0:T(8,128)(2,1)} custom-call(bf16[64,2048]{1,0:T(8,128)(2,1)} %x_in.1, bf16[64,4096,128]{2,1,0:T(8,128)(2,1)} %bitcast.k_in, bf16[64,4096,128]{2,1,0:T(8,128)(2,1)} %bitcast.1.v_in, bf16[16,128]{1,0:T(8,128)(2,1)} %bitcast.4, bf16[2048,256]{1,0:T(8,128)(2,1)} %wq_in.1, bf16[256,2048]{1,0:T(8,128)(2,1)} %wo_in.1, ...), custom_call_target="tpu_custom_call" | custom-call | tf_op jit(solution)/shard_map/layer/pallas_call | solution.py:279
  68.3 1.7 %copy.13 = bf16[64,2048]{1,0:T(8,128)(2,1)} copy(bf16[64,2048]{1,0:T(8,128)(2,1)} %layer.1) | data formatting | bytes 524288
